TPU v7x, 32 devices: a whole 2x2x4 slice. The times are simulated.
32 devices in a mesh: mem: 8 (over y, x, core), pix: 4 (over z).
Axes of the slice: x: 2, y: 2, z: 4, core: 2. Of those that a mesh axis runs over, the one named last changes fastest.
Arguments:
- prior_motion: bfloat16 [64, 16, 131072], P('mem', None, 'pix'), may hold values from -6 to 6
- measured_motion: float32 [1200], replicated, may hold values from -1.6 to 1.6
- measurement_noise_stddev: float32 [1200], replicated, may hold values from 0.05 to 0.5
- gaussian_jitter: float32 [2, 1200, 64], replicated, may hold values from -6 to 6
- scene_couples: int32 [2, 1200], replicated, may hold values from 0 to 15, as said below
- targeted_tile_number: int32 [1200], replicated, may hold values from 0 to 2047
Outputs:
- analysis: bfloat16 [64, 16, 131072], P('mem', None, 'pix')
Inputs may be any that keep to these rules, and one draw needn't show every extreme that they name: scene_couples[0, k] < scene_couples[1, k]: row 0 holds the earlier acquisition, row 1 the later.
All inputs are finite; a program needn't handle non-finite values.
Results may differ from a plain program's by a relative error of at most 0.011.
Values may be sent and summed in bfloat16 or wider, within the bound.
A program may use at most 192 MiB of HBM per device.

v0:
```python
import functools
import math

import jax
import jax.numpy as jnp
from jax import lax
from jax.experimental import pallas as pl
from jax.experimental.pallas import tpu as pltpu
from jax.sharding import PartitionSpec as P

BLK = 64
PASS_COUNT = 2
LANES = 128
CHUNKS = 4
F32 = jnp.float32
BF16 = jnp.bfloat16
HI = lax.Precision.HIGHEST
MESH = pl.DeviceIdType.MESH


def nn(a, b):
    return lax.dot_general(a, b, (((1,), (0,)), ((), ())), precision=HI, preferred_element_type=F32)


def tn(a, b):
    return nn(a.T, b)


def nt(a, b):
    return lax.dot_general(a, b, (((1,), (1,)), ((), ())), precision=HI, preferred_element_type=F32)


def iota(shape, axis):
    return lax.broadcasted_iota(jnp.int32, shape, axis)


def aligned(index, unit):
    return pl.ds(pl.multiple_of(index * unit, unit), unit)


def gauss_jordan(matrix, right, work):
    n = matrix.shape[0]
    work[...] = jnp.concatenate([matrix, right], axis=1)
    row_id = iota((n, 1), 0)
    lane_id = iota((n, 2 * n), 1)

    def step(k, carry):
        table = work[...]
        row = work[pl.ds(k, 1), :]
        here = lane_id == k
        factor = jnp.sum(jnp.where(here, table, 0.0), axis=1, keepdims=True)
        pivot = row / jnp.sum(jnp.where(here[:1], row, 0.0), axis=1, keepdims=True)
        work[...] = jnp.where(row_id == k, pivot, table - factor * pivot)
        return carry

    lax.fori_loop(0, n, step, 0)
    return work[:, n:]


def solve(total, work):
    n = total[0].shape[0]
    s, g = total[0][:, :n], total[0][:, n:]
    h1, h2 = total[1][:, :n], total[1][:, n:]
    eye = (iota((n, n), 0) == iota((n, n), 1)).astype(F32)
    m1 = gauss_jordan(eye + s / (n - 1), (g + h1 - s) / (n - 1), work).astype(BF16).astype(F32)
    m1_mean = jnp.mean(m1, axis=1, keepdims=True)
    step = eye + m1 - m1_mean
    s2 = tn(step, nn(s, step))
    g2 = tn(step, g - nn(s, jnp.broadcast_to(m1_mean, (n, n))))
    h22 = tn(step, h2)
    m2 = gauss_jordan(eye + s2 / (n - 1), (g2 + h22 - s2) / (n - 1), work).astype(BF16).astype(F32)
    m2c = m2 - jnp.mean(m2, axis=0, keepdims=True)
    w = m1 + m2 + nn(m1, m2c)
    return w - jnp.mean(w, axis=0, keepdims=True)


def expand(w, me, parts, times, mix):
    n = w.shape[0]
    members = n // parts
    rows = members * times
    depth = rows * parts
    spot = iota((n, n), 0)
    source = ((spot // members) ^ me) * members + spot % members
    order = (iota((n, n), 1) == source).astype(F32)
    wt = nt(nn(order, w.T), order)
    hi = wt.astype(BF16)
    lo = (wt - hi.astype(F32)).astype(BF16)
    spread = (iota((n, depth), 1) // times == iota((n, depth), 0)).astype(BF16)
    tall = (iota((rows, members), 0) // times == iota((rows, members), 1)).astype(BF16)
    same = iota((rows, depth), 0) % times == iota((rows, depth), 1) % times
    for piece, first in ((hi, 0), (lo, depth)):
        wide = jnp.dot(piece, spread, preferred_element_type=F32).astype(BF16)
        for part in range(parts):
            block = jnp.dot(
                tall, wide[part * members : (part + 1) * members, :], preferred_element_type=F32
            )
            start = first + part * rows
            mix[start : start + rows, :] = jnp.where(same, block, 0.0).astype(BF16)


def smoother_kernel(
    parts, tiles, times,
    prior, measured, noise, jitter, couples, target, out,
    state, fresh, mix, seen, summer, sums, work,
    measured_raw, noise_raw, couples_raw, target_raw, jitter_all,
    measured_row, noise_row, early_row, late_row, target_row,
    pred_out, pred_in, mine, members_in, stats_in,
    there_send, there_recv, back_send, back_recv,
    a_send, a_recv, b_send, b_recv, c_send, c_recv,
    look_sem, own_sem, small_sem,
):
    me = lax.axis_index("mem")
    tile = lax.axis_index("pix")
    rows, cells = prior.shape
    members = rows // times
    total_members = members * parts
    width = cells // parts
    span = width // CHUNKS
    obs = target.shape[1]
    padded = target_row.shape[1]
    share = padded // tiles
    tile_blocks = cells // BLK
    look = seen.shape[2]
    looks = cells // look

    def small(i, source, dest):
        return pltpu.make_async_copy(source, dest, small_sem.at[i])

    loads = [
        small(0, measured, measured_raw),
        small(1, noise, noise_raw),
        small(2, couples, couples_raw),
        small(3, target, target_raw),
        small(4, jitter, jitter_all.at[:, :obs, :]),
    ]

    def look_copy(i):
        return pltpu.make_async_copy(
            prior.at[:, aligned(i, look)], seen.at[lax.rem(i, 2)], look_sem.at[lax.rem(i, 2)]
        )

    own = pltpu.make_async_copy(prior.at[:, aligned(me, width)], state.at[pl.ds(0, rows), :], own_sem)

    def there(k, c):
        column = pl.multiple_of((me ^ k) * width + c * span, span)
        return pltpu.make_async_remote_copy(
            src_ref=prior.at[:, pl.ds(column, span)],
            dst_ref=state.at[pl.ds(k * rows, rows), pl.ds(c * span, span)],
            send_sem=there_send.at[k, c],
            recv_sem=there_recv.at[k, c],
            device_id={"mem": me ^ k},
            device_id_type=MESH,
        )

    def back(k, c):
        column = pl.multiple_of(me * width + c * span, span)
        return pltpu.make_async_remote_copy(
            src_ref=fresh.at[pl.ds(k * rows, rows), pl.ds(c * span, span)],
            dst_ref=out.at[:, pl.ds(column, span)],
            send_sem=back_send.at[k, c],
            recv_sem=back_recv.at[k, c],
            device_id={"mem": me ^ k},
            device_id_type=MESH,
        )

    def along(d):
        return lax.rem(tile + d, tiles)

    def send_a(d):
        return pltpu.make_async_remote_copy(
            src_ref=pred_out.at[along(d)],
            dst_ref=pred_in.at[tile],
            send_sem=a_send.at[d],
            recv_sem=a_recv.at[d],
            device_id={"pix": along(d)},
            device_id_type=MESH,
        )

    def send_b(k):
        return pltpu.make_async_remote_copy(
            src_ref=mine,
            dst_ref=members_in.at[me],
            send_sem=b_send.at[k],
            recv_sem=b_recv.at[k],
            device_id={"mem": me ^ k},
            device_id_type=MESH,
        )

    def send_c(d):
        return pltpu.make_async_remote_copy(
            src_ref=stats_in.at[tile],
            dst_ref=stats_in.at[tile],
            send_sem=c_send.at[d],
            recv_sem=c_recv.at[d],
            device_id={"pix": along(d)},
            device_id_type=MESH,
        )

    partners = list(reversed(range(1, parts)))
    others = list(range(1, tiles))

    barrier = pltpu.get_barrier_semaphore()
    for k in partners:
        pl.semaphore_signal(barrier, inc=1, device_id={"mem": me ^ k}, device_id_type=MESH)
    for d in others:
        pl.semaphore_signal(barrier, inc=1, device_id={"pix": along(d)}, device_id_type=MESH)
    look_copy(0).start()
    for load in loads:
        load.start()
    pl.semaphore_wait(barrier, len(partners) + len(others))
    for k in partners:
        there(k, 0).start()
    own.start()

    summer[...] = (iota((look, LANES), 0) // BLK == iota((look, LANES), 1)).astype(BF16)

    def look_step(i, carry):
        @pl.when(i + 1 < looks)
        def _():
            look_copy(i + 1).start()

        look_copy(i).wait()
        sums[:, aligned(i, LANES)] = jnp.dot(
            seen[lax.rem(i, 2)], summer[...], preferred_element_type=F32
        )
        return carry

    lax.fori_loop(0, looks, look_step, 0)

    for load in loads:
        load.wait()
    measured_row[...] = jnp.zeros((1, padded), F32)
    noise_row[...] = jnp.ones((1, padded), F32)
    early_row[...] = jnp.zeros((1, padded), jnp.int32)
    late_row[...] = jnp.zeros((1, padded), jnp.int32)
    target_row[...] = jnp.full((1, padded), -1, jnp.int32)
    measured_row[:, :obs] = measured_raw[...]
    noise_row[:, :obs] = noise_raw[...]
    early_row[:, :obs] = couples_raw[0:1, :]
    late_row[:, :obs] = couples_raw[1:2, :]
    target_row[:, :obs] = target_raw[...] - tile * tile_blocks
    jitter_all[:, obs:, :] = jnp.zeros((PASS_COUNT, padded - obs, total_members), F32)

    def predict(i, carry):
        lanes = aligned(i, share)
        table = (target_row[:, lanes] == iota((tile_blocks, share), 0)).astype(F32)
        part = nn(sums[...], table)
        scene = iota((rows, share), 0) % times
        pair = (scene == late_row[:, lanes]).astype(F32) - (scene == early_row[:, lanes]).astype(F32)
        group = (iota((members, rows), 1) // times == iota((members, rows), 0)).astype(F32)
        pred_out[i] = nn(group, part * pair) / BLK
        return carry

    lax.fori_loop(0, tiles, predict, 0)

    for d in others:
        send_a(d).start()
    pred_in[tile] = pred_out[tile]
    for d in others:
        send_a(d).wait()
    total = pred_in[0]
    for d in others:
        total = total + pred_in[d]
    mine[...] = total
    members_in[me] = total
    for k in partners:
        send_b(k).start()
    for c in range(1, CHUNKS):
        for k in partners:
            there(k, c).start()
    for k in partners:
        send_b(k).wait()

    pred = jnp.concatenate([members_in[i] for i in range(parts)], axis=0)
    lanes = aligned(tile, share)
    here = (iota((1, share), 1) + tile * share < obs).astype(F32)
    mean = jnp.mean(pred, axis=0, keepdims=True)
    scale = math.sqrt(float(PASS_COUNT)) * noise_row[:, lanes]
    centred = (pred - mean) / scale * here
    gap = jnp.broadcast_to((measured_row[:, lanes] - mean) / scale * here, pred.shape)
    shakes = jnp.concatenate([jitter_all[i, lanes, :] for i in range(PASS_COUNT)], axis=1)
    stats_in[tile, 0] = nt(centred, jnp.concatenate([centred, gap], axis=0))
    stats_in[tile, 1] = nn(centred, shakes)
    for d in others:
        send_c(d).start()
    for d in others:
        send_c(d).wait()
    total = stats_in[0]
    for d in others:
        total = total + stats_in[d]

    expand(solve(total, work), me, parts, times, mix)

    own.wait()
    step = math.gcd(span, 256)
    depth = parts * rows
    for c in range(CHUNKS):
        for k in partners:
            there(k, c).wait_recv()

        def update(i, carry):
            columns = pl.ds(pl.multiple_of(c * span + i * step, step), step)
            x = state[:, columns]
            both = jnp.dot(mix[...], x, preferred_element_type=F32)
            y = (x.astype(F32) + both[:depth] + both[depth:]).astype(BF16)
            fresh[:, columns] = y
            out[:, pl.ds(pl.multiple_of(me * width + c * span + i * step, step), step)] = y[:rows]
            return carry

        lax.fori_loop(0, span // step, update, 0)
        for k in partners:
            back(k, c).start()
    for c in range(CHUNKS):
        for k in partners:
            there(k, c).wait_send()
    for c in range(CHUNKS):
        for k in partners:
            back(k, c).wait()


def body(prior, measured, noise, jitter, couples, target):
    parts = lax.axis_size("mem")
    tiles = lax.axis_size("pix")
    members, times, cells = prior.shape
    total_members = members * parts
    rows = members * times
    depth = rows * parts
    width = cells // parts
    obs = target.shape[0]
    unit = LANES * tiles
    padded = obs + (-obs) % unit
    share = padded // tiles
    look = LANES * BLK
    anywhere = pl.BlockSpec(memory_space=pl.ANY)
    dma = pltpu.SemaphoreType.DMA
    scratch = [
        pltpu.VMEM((depth, width), BF16),
        pltpu.VMEM((depth, width), BF16),
        pltpu.VMEM((2 * depth, depth), BF16),
        pltpu.VMEM((2, rows, look), BF16),
        pltpu.VMEM((look, LANES), BF16),
        pltpu.VMEM((rows, cells // BLK), F32),
        pltpu.VMEM((total_members, 2 * total_members), F32),
        pltpu.VMEM((1, obs), F32),
        pltpu.VMEM((1, obs), F32),
        pltpu.VMEM((2, obs), jnp.int32),
        pltpu.VMEM((1, obs), jnp.int32),
        pltpu.VMEM((PASS_COUNT, padded, total_members), F32),
        pltpu.VMEM((1, padded), F32),
        pltpu.VMEM((1, padded), F32),
        pltpu.VMEM((1, padded), jnp.int32),
        pltpu.VMEM((1, padded), jnp.int32),
        pltpu.VMEM((1, padded), jnp.int32),
        pltpu.VMEM((tiles, members, share), F32),
        pltpu.VMEM((tiles, members, share), F32),
        pltpu.VMEM((members, share), F32),
        pltpu.VMEM((parts, members, share), F32),
        pltpu.VMEM((tiles, 2, total_members, 2 * total_members), F32),
        dma((parts, CHUNKS)),
        dma((parts, CHUNKS)),
        dma((parts, CHUNKS)),
        dma((parts, CHUNKS)),
        dma((tiles,)),
        dma((tiles,)),
        dma((parts,)),
        dma((parts,)),
        dma((tiles,)),
        dma((tiles,)),
        dma((2,)),
        dma,
        dma((5,)),
    ]
    out = pl.pallas_call(
        functools.partial(smoother_kernel, parts, tiles, times),
        in_specs=[anywhere] * 6,
        out_specs=pl.BlockSpec(memory_space=pltpu.VMEM),
        out_shape=jax.ShapeDtypeStruct((rows, cells), BF16),
        scratch_shapes=scratch,
        compiler_params=pltpu.CompilerParams(
            collective_id=0, has_side_effects=True, vmem_limit_bytes=52 * 1024 * 1024
        ),
        name="smoother",
    )(prior.reshape(rows, cells), measured[None, :], noise[None, :], jitter, couples, target[None, :])
    return out.reshape(prior.shape)


def solution(mesh):
    return jax.shard_map(
        body,
        mesh=mesh,
        in_specs=(P("mem", None, "pix"), P(), P(), P(), P(), P()),
        out_specs=P("mem", None, "pix"),
        check_vma=False,
    )
```

profile of v0, /device:TPU:0, one launch (start us, length us, event | category | flops | bytes accessed | tf_op | source)
XLA Modules:
  0.0 204.9 jit_solution(10593673743125928785)
XLA Ops:
  0.0 0.7 broadcast_in_dim.9.measured
  0.7 0.7 broadcast_in_dim.10.noise
  1.4 0.7 broadcast_in_dim.11.target
  2.1 1.5 copy.7.jitter
  3.6 0.0 copy-start
  3.6 0.7 copy-done
  4.3 193.0 %smoother.1 = bf16[128,32768]{1,0:T(8,128)(2,1)} custom-call(bf16[128,32768]{1,0:T(8,128)(2,1)} %bitcast.3, f32[1,1200]{1,0:T(1,128)S(1)} %broadcast_in_dim.9.measured, f32[1,1200]{1,0:T(1,128)S(1)} %broadcast_in_dim.10.noise, f32[2,1200,64]{2,1,0:T(8,128)S(1)} %copy.7.jitter, s32[2,1200]{1,0:T(2,128)S(1)} %copy-done, s32[1,1200]{1,0:T(1,128)S(1)} %broadcast_in_dim.11.target), custom_call_target="tpu_custom_call" | custom-call | tf_op jit(solution)/shard_map/smoother/pallas_call | solution.py:373
  197.3 7.5 %copy.9 = bf16[8,16,32768]{2,1,0:T(8,128)(2,1)} copy(bf16[8,16,32768]{2,1,0:T(8,128)(2,1)} %bitcast.2) | data formatting | bytes 16777216
Async XLA Ops:
  3.6 0.7 copy-start
where the time goes:
time: 205 us
  Pallas kernels  193 us (94%)
  local copies, waits for them, and re-layouts  11.8 us (6%)
    pallas_call x1, Pallas kernels, body(): pl.pallas_call(functools.partial(smoother_kernel, parts, tiles, times), i...  193 us
    unnamed x4, local copies, waits for them, and re-layouts  9.69 us

commit v1 on v0

--- a/solution.py
+++ b/solution.py
@@ -101,8 +101,8 @@
 def smoother_kernel(
     parts, tiles, times,
     prior, measured, noise, jitter, couples, target, out,
-    state, fresh, mix, seen, summer, sums, work,
-    measured_raw, noise_raw, couples_raw, target_raw, jitter_all,
+    state, mix, seen, summer, sums, work,
+    measured_raw, noise_raw, couples_raw, target_raw, jitter_raw, jitter_all,
     measured_row, noise_row, early_row, late_row, target_row,
     pred_out, pred_in, mine, members_in, stats_in,
     there_send, there_recv, back_send, back_recv,
@@ -116,7 +116,7 @@
     total_members = members * parts
     width = cells // parts
     span = width // CHUNKS
-    obs = target.shape[1]
+    obs = target.shape[0]
     padded = target_row.shape[1]
     share = padded // tiles
     tile_blocks = cells // BLK
@@ -131,7 +131,7 @@
         small(1, noise, noise_raw),
         small(2, couples, couples_raw),
         small(3, target, target_raw),
-        small(4, jitter, jitter_all.at[:, :obs, :]),
+        small(4, jitter, jitter_raw),
     ]
 
     def look_copy(i):
@@ -155,7 +155,7 @@
     def back(k, c):
         column = pl.multiple_of(me * width + c * span, span)
         return pltpu.make_async_remote_copy(
-            src_ref=fresh.at[pl.ds(k * rows, rows), pl.ds(c * span, span)],
+            src_ref=state.at[pl.ds(k * rows, rows), pl.ds(c * span, span)],
             dst_ref=out.at[:, pl.ds(column, span)],
             send_sem=back_send.at[k, c],
             recv_sem=back_recv.at[k, c],
@@ -234,12 +234,13 @@
     early_row[...] = jnp.zeros((1, padded), jnp.int32)
     late_row[...] = jnp.zeros((1, padded), jnp.int32)
     target_row[...] = jnp.full((1, padded), -1, jnp.int32)
-    measured_row[:, :obs] = measured_raw[...]
-    noise_row[:, :obs] = noise_raw[...]
+    measured_row[:, :obs] = measured_raw[...].reshape(1, obs)
+    noise_row[:, :obs] = noise_raw[...].reshape(1, obs)
     early_row[:, :obs] = couples_raw[0:1, :]
     late_row[:, :obs] = couples_raw[1:2, :]
-    target_row[:, :obs] = target_raw[...] - tile * tile_blocks
-    jitter_all[:, obs:, :] = jnp.zeros((PASS_COUNT, padded - obs, total_members), F32)
+    target_row[:, :obs] = target_raw[...].reshape(1, obs) - tile * tile_blocks
+    jitter_all[...] = jnp.zeros((PASS_COUNT, total_members, padded), F32)
+    jitter_all[:, :, :obs] = jitter_raw[...]
 
     def predict(i, carry):
         lanes = aligned(i, share)
@@ -278,9 +279,9 @@
     scale = math.sqrt(float(PASS_COUNT)) * noise_row[:, lanes]
     centred = (pred - mean) / scale * here
     gap = jnp.broadcast_to((measured_row[:, lanes] - mean) / scale * here, pred.shape)
-    shakes = jnp.concatenate([jitter_all[i, lanes, :] for i in range(PASS_COUNT)], axis=1)
     stats_in[tile, 0] = nt(centred, jnp.concatenate([centred, gap], axis=0))
-    stats_in[tile, 1] = nn(centred, shakes)
+    shakes = jnp.concatenate([jitter_all[i, :, lanes] for i in range(PASS_COUNT)], axis=0)
+    stats_in[tile, 1] = nt(centred, shakes)
     for d in others:
         send_c(d).start()
     for d in others:
@@ -303,7 +304,7 @@
             x = state[:, columns]
             both = jnp.dot(mix[...], x, preferred_element_type=F32)
             y = (x.astype(F32) + both[:depth] + both[depth:]).astype(BF16)
-            fresh[:, columns] = y
+            state[:, columns] = y
             out[:, pl.ds(pl.multiple_of(me * width + c * span + i * step, step), step)] = y[:rows]
             return carry
 
@@ -331,21 +332,21 @@
     padded = obs + (-obs) % unit
     share = padded // tiles
     look = LANES * BLK
-    anywhere = pl.BlockSpec(memory_space=pl.ANY)
+    far = pl.BlockSpec(memory_space=pltpu.HBM)
     dma = pltpu.SemaphoreType.DMA
     scratch = [
-        pltpu.VMEM((depth, width), BF16),
         pltpu.VMEM((depth, width), BF16),
         pltpu.VMEM((2 * depth, depth), BF16),
         pltpu.VMEM((2, rows, look), BF16),
         pltpu.VMEM((look, LANES), BF16),
         pltpu.VMEM((rows, cells // BLK), F32),
         pltpu.VMEM((total_members, 2 * total_members), F32),
-        pltpu.VMEM((1, obs), F32),
-        pltpu.VMEM((1, obs), F32),
+        pltpu.VMEM((obs,), F32),
+        pltpu.VMEM((obs,), F32),
         pltpu.VMEM((2, obs), jnp.int32),
-        pltpu.VMEM((1, obs), jnp.int32),
-        pltpu.VMEM((PASS_COUNT, padded, total_members), F32),
+        pltpu.VMEM((obs,), jnp.int32),
+        pltpu.VMEM((PASS_COUNT, total_members, obs), F32),
+        pltpu.VMEM((PASS_COUNT, total_members, padded), F32),
         pltpu.VMEM((1, padded), F32),
         pltpu.VMEM((1, padded), F32),
         pltpu.VMEM((1, padded), jnp.int32),
@@ -370,17 +371,25 @@
         dma,
         dma((5,)),
     ]
+    operands = (
+        prior.reshape(rows, cells),
+        measured,
+        noise,
+        jnp.swapaxes(jitter, 1, 2),
+        couples,
+        target,
+    )
     out = pl.pallas_call(
         functools.partial(smoother_kernel, parts, tiles, times),
-        in_specs=[anywhere] * 6,
+        in_specs=[far] * 6,
         out_specs=pl.BlockSpec(memory_space=pltpu.VMEM),
-        out_shape=jax.ShapeDtypeStruct((rows, cells), BF16),
+        out_shape=pltpu.VMEM((rows, cells), BF16),
         scratch_shapes=scratch,
         compiler_params=pltpu.CompilerParams(
-            collective_id=0, has_side_effects=True, vmem_limit_bytes=52 * 1024 * 1024
+            collective_id=0, has_side_effects=True, vmem_limit_bytes=44 * 1024 * 1024
         ),
         name="smoother",
-    )(prior.reshape(rows, cells), measured[None, :], noise[None, :], jitter, couples, target[None, :])
+    )(*(pltpu.with_memory_space_constraint(a, pltpu.HBM) for a in operands))
     return out.reshape(prior.shape)
 
 

time: 205 us -> 193 us (0.941)
  local copies, waits for them, and re-layouts: 11.8 us -> 3.4 us
  Pallas kernels: 193 us -> 190 us
    unnamed x4 -> x1, local copies, waits for them, and re-layouts: 9.69 us -> 3.4 us
    pallas_call x1, Pallas kernels: 193 us -> 190 us  [body(): pl.pallas_call(functools.partial(smoother_kernel, parts, tiles, times), i...]
    broadcast_in_dim x3 -> x0, local copies, waits for them, and re-layouts: 2.1 us -> none  [the longest x1 0.7 us: body(): measured[None, :]]
where the time goes in v1:
time: 193 us
  Pallas kernels  190 us (98%)
  local copies, waits for them, and re-layouts  3.4 us (2%)
    pallas_call x1, Pallas kernels, body(): pl.pallas_call(functools.partial(smoother_kernel, parts, tiles, times), i...  190 us

profile of v1, /device:TPU:0, one launch (start us, length us, event | category | flops | bytes accessed | tf_op | source)
XLA Modules:
  0.0 193.2 jit_solution(15011107287894854558)
XLA Ops:
  0.0 189.8 %smoother.1 = bf16[128,32768]{1,0:T(8,128)(2,1)S(1)} custom-call(bf16[128,32768]{1,0:T(8,128)(2,1)} %bitcast.4, f32[1200]{0:T(1024)} %measured.1, f32[1200]{0:T(1024)} %noise.1, f32[2,64,1200]{2,1,0:T(8,128)} %bitcast.5, s32[2,1200]{1,0:T(2,128)} %couples.1, s32[1200]{0:T(1024)} %target.1), custom_call_target="tpu_custom_call" | custom-call | tf_op jit(solution)/shard_map/smoother/pallas_call | solution.py:382
  189.8 3.4 %copy.8 = bf16[8,16,32768]{2,1,0:T(8,128)(2,1)} copy(bf16[8,16,32768]{2,1,0:T(8,128)(2,1)S(1)} %bitcast.3) | data formatting | bytes 16777216

commit v2 on v1

--- a/solution.py
+++ b/solution.py
@@ -106,8 +106,8 @@
     measured_row, noise_row, early_row, late_row, target_row,
     pred_out, pred_in, mine, members_in, stats_in,
     there_send, there_recv, back_send, back_recv,
-    a_send, a_recv, b_send, b_recv, c_send, c_recv,
-    look_sem, own_sem, small_sem,
+    a_send, a_recv, b_send, b_recv, r_send, r_recv, c_send, c_recv,
+    look_sem, own_sem, small_sem, go_sem,
 ):
     me = lax.axis_index("mem")
     tile = lax.axis_index("pix")
@@ -186,6 +186,16 @@
             device_id_type=MESH,
         )
 
+    def relay(k):
+        return pltpu.make_async_remote_copy(
+            src_ref=members_in.at[me ^ k],
+            dst_ref=members_in.at[me ^ k],
+            send_sem=r_send.at[k],
+            recv_sem=r_recv.at[k],
+            device_id={"mem": me ^ 1},
+            device_id_type=MESH,
+        )
+
     def send_c(d):
         return pltpu.make_async_remote_copy(
             src_ref=stats_in.at[tile],
@@ -197,17 +207,32 @@
         )
 
     partners = list(reversed(range(1, parts)))
+    evens = partners[1::2]
     others = list(range(1, tiles))
 
     barrier = pltpu.get_barrier_semaphore()
     for k in partners:
         pl.semaphore_signal(barrier, inc=1, device_id={"mem": me ^ k}, device_id_type=MESH)
-    for d in others:
-        pl.semaphore_signal(barrier, inc=1, device_id={"pix": along(d)}, device_id_type=MESH)
     look_copy(0).start()
     for load in loads:
         load.start()
-    pl.semaphore_wait(barrier, len(partners) + len(others))
+
+    @pl.when(me != parts - 1)
+    def _():
+        pl.semaphore_wait(barrier, len(partners))
+
+    @pl.when(me == parts - 2)
+    def _():
+        for d in others:
+            there_id = {"mem": parts - 1, "pix": along(d)}
+            pl.semaphore_signal(barrier, inc=1, device_id=there_id, device_id_type=MESH)
+
+    @pl.when(me == parts - 1)
+    def _():
+        pl.semaphore_wait(barrier, len(partners) + len(others))
+        for k in partners:
+            pl.semaphore_signal(go_sem, inc=1, device_id={"mem": me ^ k}, device_id_type=MESH)
+
     for k in partners:
         there(k, 0).start()
     own.start()
@@ -254,6 +279,10 @@
 
     lax.fori_loop(0, tiles, predict, 0)
 
+    @pl.when(me != parts - 1)
+    def _():
+        pl.semaphore_wait(go_sem, 1)
+
     for d in others:
         send_a(d).start()
     pred_in[tile] = pred_out[tile]
@@ -264,13 +293,17 @@
         total = total + pred_in[d]
     mine[...] = total
     members_in[me] = total
-    for k in partners:
+    for k in evens + [1]:
         send_b(k).start()
     for c in range(1, CHUNKS):
         for k in partners:
             there(k, c).start()
-    for k in partners:
+    for k in evens:
         send_b(k).wait()
+        relay(k).start()
+    send_b(1).wait()
+    for k in evens:
+        relay(k).wait()
 
     pred = jnp.concatenate([members_in[i] for i in range(parts)], axis=0)
     lanes = aligned(tile, share)
@@ -365,11 +398,14 @@
         dma((tiles,)),
         dma((parts,)),
         dma((parts,)),
+        dma((parts,)),
+        dma((parts,)),
         dma((tiles,)),
         dma((tiles,)),
         dma((2,)),
         dma,
         dma((5,)),
+        pltpu.SemaphoreType.REGULAR,
     ]
     operands = (
         prior.reshape(rows, cells),

time: 193 us -> 191 us (0.990)
  Pallas kernels: 190 us -> 188 us
where the time goes in v2:
time: 191 us
  Pallas kernels  188 us (98%)
  local copies, waits for them, and re-layouts  3.4 us (2%)
    pallas_call x1, Pallas kernels, body(): pl.pallas_call(functools.partial(smoother_kernel, parts, tiles, times), i...  188 us

profile of v2, /device:TPU:0, one launch (start us, length us, event | category | flops | bytes accessed | tf_op | source)
XLA Modules:
  0.0 191.3 jit_solution(18162715652168961586)
XLA Ops:
  0.0 187.9 %smoother.1 = bf16[128,32768]{1,0:T(8,128)(2,1)S(1)} custom-call(bf16[128,32768]{1,0:T(8,128)(2,1)} %bitcast.4, f32[1200]{0:T(1024)} %measured.1, f32[1200]{0:T(1024)} %noise.1, f32[2,64,1200]{2,1,0:T(8,128)} %bitcast.5, s32[2,1200]{1,0:T(2,128)} %couples.1, s32[1200]{0:T(1024)} %target.1), custom_call_target="tpu_custom_call" | custom-call | tf_op jit(solution)/shard_map/smoother/pallas_call | solution.py:418
  187.9 3.4 %copy.8 = bf16[8,16,32768]{2,1,0:T(8,128)(2,1)} copy(bf16[8,16,32768]{2,1,0:T(8,128)(2,1)S(1)} %bitcast.3) | data formatting | bytes 16777216

commit v3 on v2

--- a/solution.py
+++ b/solution.py
@@ -217,19 +217,24 @@
     for load in loads:
         load.start()
 
-    @pl.when(me != parts - 1)
+    speaker = me == parts - 1
+    root = jnp.logical_and(speaker, tile == tiles - 1)
+    branch = jnp.logical_and(speaker, tile != tiles - 1)
+
+    @pl.when(jnp.logical_not(root))
     def _():
         pl.semaphore_wait(barrier, len(partners))
 
-    @pl.when(me == parts - 2)
+    @pl.when(branch)
     def _():
-        for d in others:
-            there_id = {"mem": parts - 1, "pix": along(d)}
-            pl.semaphore_signal(barrier, inc=1, device_id=there_id, device_id_type=MESH)
-
-    @pl.when(me == parts - 1)
+        root_id = {"mem": me, "pix": tiles - 1}
+        pl.semaphore_signal(barrier, inc=1, device_id=root_id, device_id_type=MESH)
+
+    @pl.when(root)
     def _():
         pl.semaphore_wait(barrier, len(partners) + len(others))
+        for d in others:
+            pl.semaphore_signal(go_sem, inc=1, device_id={"pix": along(d)}, device_id_type=MESH)
         for k in partners:
             pl.semaphore_signal(go_sem, inc=1, device_id={"mem": me ^ k}, device_id_type=MESH)
 
@@ -279,9 +284,14 @@
 
     lax.fori_loop(0, tiles, predict, 0)
 
-    @pl.when(me != parts - 1)
+    @pl.when(jnp.logical_not(root))
     def _():
         pl.semaphore_wait(go_sem, 1)
+
+    @pl.when(branch)
+    def _():
+        for k in partners:
+            pl.semaphore_signal(go_sem, inc=1, device_id={"mem": me ^ k}, device_id_type=MESH)
 
     for d in others:
         send_a(d).start()

time: 191 us -> 191 us (level)
  no operation moved by 1% of the time
where the time goes in v3:
time: 191 us
  Pallas kernels  188 us (98%)
  local copies, waits for them, and re-layouts  3.4 us (2%)
    pallas_call x1, Pallas kernels, body(): pl.pallas_call(functools.partial(smoother_kernel, parts, tiles, times), i...  188 us

profile of v3, /device:TPU:0, one launch (start us, length us, event | category | flops | bytes accessed | tf_op | source)
XLA Modules:
  0.0 191.3 jit_solution(15408099574828893901)
XLA Ops:
  0.0 187.9 %smoother.1 = bf16[128,32768]{1,0:T(8,128)(2,1)S(1)} custom-call(bf16[128,32768]{1,0:T(8,128)(2,1)} %bitcast.4, f32[1200]{0:T(1024)} %measured.1, f32[1200]{0:T(1024)} %noise.1, f32[2,64,1200]{2,1,0:T(8,128)} %bitcast.5, s32[2,1200]{1,0:T(2,128)} %couples.1, s32[1200]{0:T(1024)} %target.1), custom_call_target="tpu_custom_call" | custom-call | tf_op jit(solution)/shard_map/smoother/pallas_call | solution.py:428
  187.9 3.4 %copy.8 = bf16[8,16,32768]{2,1,0:T(8,128)(2,1)} copy(bf16[8,16,32768]{2,1,0:T(8,128)(2,1)S(1)} %bitcast.3) | data formatting | bytes 16777216

commit v4 on v3

--- a/solution.py
+++ b/solution.py
@@ -146,8 +146,8 @@
         return pltpu.make_async_remote_copy(
             src_ref=prior.at[:, pl.ds(column, span)],
             dst_ref=state.at[pl.ds(k * rows, rows), pl.ds(c * span, span)],
-            send_sem=there_send.at[k, c],
-            recv_sem=there_recv.at[k, c],
+            send_sem=there_send,
+            recv_sem=there_recv.at[c],
             device_id={"mem": me ^ k},
             device_id_type=MESH,
         )
@@ -157,8 +157,8 @@
         return pltpu.make_async_remote_copy(
             src_ref=state.at[pl.ds(k * rows, rows), pl.ds(c * span, span)],
             dst_ref=out.at[:, pl.ds(column, span)],
-            send_sem=back_send.at[k, c],
-            recv_sem=back_recv.at[k, c],
+            send_sem=back_send,
+            recv_sem=back_recv,
             device_id={"mem": me ^ k},
             device_id_type=MESH,
         )
@@ -170,8 +170,8 @@
         return pltpu.make_async_remote_copy(
             src_ref=pred_out.at[along(d)],
             dst_ref=pred_in.at[tile],
-            send_sem=a_send.at[d],
-            recv_sem=a_recv.at[d],
+            send_sem=a_send,
+            recv_sem=a_recv,
             device_id={"pix": along(d)},
             device_id_type=MESH,
         )
@@ -180,8 +180,8 @@
         return pltpu.make_async_remote_copy(
             src_ref=mine,
             dst_ref=members_in.at[me],
-            send_sem=b_send.at[k],
-            recv_sem=b_recv.at[k],
+            send_sem=b_send,
+            recv_sem=b_recv,
             device_id={"mem": me ^ k},
             device_id_type=MESH,
         )
@@ -190,8 +190,8 @@
         return pltpu.make_async_remote_copy(
             src_ref=members_in.at[me ^ k],
             dst_ref=members_in.at[me ^ k],
-            send_sem=r_send.at[k],
-            recv_sem=r_recv.at[k],
+            send_sem=r_send,
+            recv_sem=r_recv,
             device_id={"mem": me ^ 1},
             device_id_type=MESH,
         )
@@ -200,9 +200,19 @@
         return pltpu.make_async_remote_copy(
             src_ref=stats_in.at[tile],
             dst_ref=stats_in.at[tile],
-            send_sem=c_send.at[d],
-            recv_sem=c_recv.at[d],
+            send_sem=c_send,
+            recv_sem=c_recv,
             device_id={"pix": along(d)},
+            device_id_type=MESH,
+        )
+
+    def whole(region, send_sem, recv_sem):
+        return pltpu.make_async_remote_copy(
+            src_ref=region,
+            dst_ref=region,
+            send_sem=send_sem,
+            recv_sem=recv_sem,
+            device_id={"mem": me ^ 1},
             device_id_type=MESH,
         )
 
@@ -296,8 +306,7 @@
     for d in others:
         send_a(d).start()
     pred_in[tile] = pred_out[tile]
-    for d in others:
-        send_a(d).wait()
+    whole(pred_in.at[pl.ds(0, len(others))], a_send, a_recv).wait()
     total = pred_in[0]
     for d in others:
         total = total + pred_in[d]
@@ -308,12 +317,10 @@
     for c in range(1, CHUNKS):
         for k in partners:
             there(k, c).start()
+    whole(members_in.at[pl.ds(0, len(evens) + 1)], b_send, b_recv).wait()
     for k in evens:
-        send_b(k).wait()
         relay(k).start()
-    send_b(1).wait()
-    for k in evens:
-        relay(k).wait()
+    whole(members_in.at[pl.ds(0, len(evens))], r_send, r_recv).wait()
 
     pred = jnp.concatenate([members_in[i] for i in range(parts)], axis=0)
     lanes = aligned(tile, share)
@@ -327,8 +334,7 @@
     stats_in[tile, 1] = nt(centred, shakes)
     for d in others:
         send_c(d).start()
-    for d in others:
-        send_c(d).wait()
+    whole(stats_in.at[pl.ds(0, len(others))], c_send, c_recv).wait()
     total = stats_in[0]
     for d in others:
         total = total + stats_in[d]
@@ -339,8 +345,8 @@
     step = math.gcd(span, 256)
     depth = parts * rows
     for c in range(CHUNKS):
-        for k in partners:
-            there(k, c).wait_recv()
+        arrived = state.at[pl.ds(rows, depth - rows), pl.ds(c * span, span)]
+        whole(arrived, there_send, there_recv.at[c]).wait_recv()
 
         def update(i, carry):
             columns = pl.ds(pl.multiple_of(c * span + i * step, step), step)
@@ -354,12 +360,9 @@
         lax.fori_loop(0, span // step, update, 0)
         for k in partners:
             back(k, c).start()
-    for c in range(CHUNKS):
-        for k in partners:
-            there(k, c).wait_send()
-    for c in range(CHUNKS):
-        for k in partners:
-            back(k, c).wait()
+    moved = state.at[pl.ds(rows, depth - rows), :]
+    whole(moved, there_send, back_recv).wait_send()
+    whole(moved, back_send, back_recv).wait()
 
 
 def body(prior, measured, noise, jitter, couples, target):
@@ -400,18 +403,18 @@
         pltpu.VMEM((members, share), F32),
         pltpu.VMEM((parts, members, share), F32),
         pltpu.VMEM((tiles, 2, total_members, 2 * total_members), F32),
-        dma((parts, CHUNKS)),
-        dma((parts, CHUNKS)),
-        dma((parts, CHUNKS)),
-        dma((parts, CHUNKS)),
-        dma((tiles,)),
-        dma((tiles,)),
-        dma((parts,)),
-        dma((parts,)),
-        dma((parts,)),
-        dma((parts,)),
-        dma((tiles,)),
-        dma((tiles,)),
+        dma,
+        dma((CHUNKS,)),
+        dma,
+        dma,
+        dma,
+        dma,
+        dma,
+        dma,
+        dma,
+        dma,
+        dma,
+        dma,
         dma((2,)),
         dma,
         dma((5,)),

time: 191 us -> 190 us (level)
  Pallas kernels: 188 us -> 186 us
where the time goes in v4:
time: 190 us
  Pallas kernels  186 us (98%)
  local copies, waits for them, and re-layouts  3.4 us (2%)
    pallas_call x1, Pallas kernels, body(): pl.pallas_call(functools.partial(smoother_kernel, parts, tiles, times), i...  186 us

profile of v4, /device:TPU:0, one launch (start us, length us, event | category | flops | bytes accessed | tf_op | source)
XLA Modules:
  0.0 189.9 jit_solution(14272035153420338877)
XLA Ops:
  0.0 186.5 %smoother.1 = bf16[128,32768]{1,0:T(8,128)(2,1)S(1)} custom-call(bf16[128,32768]{1,0:T(8,128)(2,1)} %bitcast.4, f32[1200]{0:T(1024)} %measured.1, f32[1200]{0:T(1024)} %noise.1, f32[2,64,1200]{2,1,0:T(8,128)} %bitcast.5, s32[2,1200]{1,0:T(2,128)} %couples.1, s32[1200]{0:T(1024)} %target.1), custom_call_target="tpu_custom_call" | custom-call | tf_op jit(solution)/shard_map/smoother/pallas_call | solution.py:431
  186.5 3.4 %copy.8 = bf16[8,16,32768]{2,1,0:T(8,128)(2,1)} copy(bf16[8,16,32768]{2,1,0:T(8,128)(2,1)S(1)} %bitcast.3) | data formatting | bytes 16777216

commit v5 on v4

--- a/solution.py
+++ b/solution.py
@@ -100,12 +100,12 @@
 
 def smoother_kernel(
     parts, tiles, times,
-    prior, measured, noise, jitter, couples, target, out,
+    prior, measured, noise, jitter, couples, target, out, rest, last,
     state, mix, seen, summer, sums, work,
     measured_raw, noise_raw, couples_raw, target_raw, jitter_raw, jitter_all,
     measured_row, noise_row, early_row, late_row, target_row,
     pred_out, pred_in, mine, members_in, stats_in,
-    there_send, there_recv, back_send, back_recv,
+    there_send, there_recv, back_send, back_recv, early_send, early_recv,
     a_send, a_recv, b_send, b_recv, r_send, r_recv, c_send, c_recv,
     look_sem, own_sem, small_sem, go_sem,
 ):
@@ -153,12 +153,22 @@
         )
 
     def back(k, c):
-        column = pl.multiple_of(me * width + c * span, span)
+        column = pl.multiple_of(me * (width - span) + c * span, span)
         return pltpu.make_async_remote_copy(
             src_ref=state.at[pl.ds(k * rows, rows), pl.ds(c * span, span)],
             dst_ref=out.at[:, pl.ds(column, span)],
             send_sem=back_send,
             recv_sem=back_recv,
+            device_id={"mem": me ^ k},
+            device_id_type=MESH,
+        )
+
+    def early(k):
+        return pltpu.make_async_remote_copy(
+            src_ref=last.at[pl.ds(k * rows, rows), :],
+            dst_ref=rest.at[:, aligned(me, span)],
+            send_sem=early_send,
+            recv_sem=early_recv,
             device_id={"mem": me ^ k},
             device_id_type=MESH,
         )
@@ -353,16 +363,118 @@
             x = state[:, columns]
             both = jnp.dot(mix[...], x, preferred_element_type=F32)
             y = (x.astype(F32) + both[:depth] + both[depth:]).astype(BF16)
-            state[:, columns] = y
-            out[:, pl.ds(pl.multiple_of(me * width + c * span + i * step, step), step)] = y[:rows]
+            if c < CHUNKS - 1:
+                state[:, columns] = y
+                column = me * (width - span) + c * span + i * step
+                out[:, pl.ds(pl.multiple_of(column, step), step)] = y[:rows]
+            else:
+                last[:, aligned(i, step)] = y
+                rest[:, pl.ds(pl.multiple_of(me * span + i * step, step), step)] = y[:rows]
             return carry
 
         lax.fori_loop(0, span // step, update, 0)
-        for k in partners:
-            back(k, c).start()
-    moved = state.at[pl.ds(rows, depth - rows), :]
-    whole(moved, there_send, back_recv).wait_send()
+        if c < CHUNKS - 1:
+            for k in partners:
+                back(k, c).start()
+
+    odd = lax.rem(me, 2) == 1
+
+    @pl.when(odd)
+    def _():
+        for k in evens:
+            early(k).start()
+
+    whole(state.at[pl.ds(rows, depth - rows), :], there_send, back_recv).wait_send()
+    moved = state.at[pl.ds(rows, depth - rows), pl.ds(0, width - span)]
     whole(moved, back_send, back_recv).wait()
+
+    @pl.when(odd)
+    def _():
+        whole(last.at[pl.ds(0, len(evens) * rows), :], early_send, early_recv).wait()
+
+
+def finish_kernel(parts, out_early, rest, last, out, send_sem, recv_sem, go_sem):
+    me = lax.axis_index("mem")
+    rows = rest.shape[0]
+    span = last.shape[1]
+    partners = list(reversed(range(1, parts)))
+    evens = partners[1::2]
+    odds = partners[0::2]
+    odd = lax.rem(me, 2) == 1
+    even = jnp.logical_not(odd)
+    barrier = pltpu.get_barrier_semaphore()
+
+    def copy(k):
+        return pltpu.make_async_remote_copy(
+            src_ref=last.at[pl.ds(k * rows, rows), :],
+            dst_ref=out.at[:, aligned(me, span)],
+            send_sem=send_sem,
+            recv_sem=recv_sem,
+            device_id={"mem": me ^ k},
+            device_id_type=MESH,
+        )
+
+    def signal(sem, k):
+        pl.semaphore_signal(sem, inc=1, device_id={"mem": me ^ k}, device_id_type=MESH)
+
+    def settle(count):
+        region = last.at[pl.ds(0, count * rows), :]
+        pltpu.make_async_remote_copy(
+            src_ref=region,
+            dst_ref=region,
+            send_sem=send_sem,
+            recv_sem=recv_sem,
+            device_id={"mem": me ^ 1},
+            device_id_type=MESH,
+        ).wait()
+
+    for k in evens:
+        signal(barrier, k)
+
+    @pl.when(even)
+    def _():
+        for k in odds:
+            signal(barrier, k)
+        pl.semaphore_wait(barrier, len(evens))
+        for k in evens:
+            copy(k).start()
+        pl.semaphore_wait(go_sem, len(odds))
+
+    @pl.when(odd)
+    def _():
+        pl.semaphore_wait(barrier, len(partners))
+        for k in odds:
+            signal(go_sem, k)
+
+    for k in odds:
+        copy(k).start()
+    out[:, aligned(me, span)] = rest[:, aligned(me, span)]
+
+    @pl.when(odd)
+    def _():
+        for k in evens:
+            out[:, aligned(me ^ k, span)] = rest[:, aligned(me ^ k, span)]
+        settle(len(odds))
+
+    @pl.when(even)
+    def _():
+        settle(len(partners))
+
+
+def write_kernel(parts, width, offset, piece, out, sem):
+    size = piece.shape[1] // parts
+    copies = [
+        pltpu.make_async_copy(
+            piece.at[:, pl.ds(i * size, size)],
+            out.at[:, pl.ds(i * width + offset, size)],
+            sem.at[i],
+        )
+        for i in range(parts)
+    ]
+    for copy in copies:
+        copy.start()
+    for copy in copies:
+        copy.wait()
 
 
 def body(prior, measured, noise, jitter, couples, target):
@@ -415,6 +527,8 @@
         dma,
         dma,
         dma,
+        dma,
+        dma,
         dma((2,)),
         dma,
         dma((5,)),
@@ -428,17 +542,57 @@
         couples,
         target,
     )
-    out = pl.pallas_call(
+    span = width // CHUNKS
+    near = pl.BlockSpec(memory_space=pltpu.VMEM)
+    most, rest, last = pl.pallas_call(
         functools.partial(smoother_kernel, parts, tiles, times),
         in_specs=[far] * 6,
-        out_specs=pl.BlockSpec(memory_space=pltpu.VMEM),
-        out_shape=pltpu.VMEM((rows, cells), BF16),
+        out_specs=[near] * 3,
+        out_shape=[
+            pltpu.VMEM((rows, parts * (width - span)), BF16),
+            pltpu.VMEM((rows, parts * span), BF16),
+            pltpu.VMEM((depth, span), BF16),
+        ],
         scratch_shapes=scratch,
         compiler_params=pltpu.CompilerParams(
             collective_id=0, has_side_effects=True, vmem_limit_bytes=44 * 1024 * 1024
         ),
         name="smoother",
     )(*(pltpu.with_memory_space_constraint(a, pltpu.HBM) for a in operands))
+    out = pl.pallas_call(
+        functools.partial(write_kernel, parts, width, 0),
+        in_specs=[near],
+        out_specs=far,
+        out_shape=pltpu.HBM((rows, cells), BF16),
+        scratch_shapes=[dma((parts,))],
+        compiler_params=pltpu.CompilerParams(vmem_limit_bytes=4 * 1024 * 1024),
+        name="write_most",
+    )(most)
+    rest = pl.pallas_call(
+        functools.partial(finish_kernel, parts),
+        in_specs=[far, near, near],
+        out_specs=near,
+        out_shape=pltpu.VMEM((rows, parts * span), BF16),
+        scratch_shapes=[dma, dma, pltpu.SemaphoreType.REGULAR],
+        compiler_params=pltpu.CompilerParams(
+            collective_id=1, has_side_effects=True, vmem_limit_bytes=8 * 1024 * 1024
+        ),
+        name="finish",
+    )(pltpu.with_memory_space_constraint(out, pltpu.HBM), rest, last)
+
+    def write_rest(piece, before, after, sem):
+        write_kernel(parts, width, width - span, piece, after, sem)
+
+    out = pl.pallas_call(
+        write_rest,
+        in_specs=[near, far],
+        out_specs=far,
+        out_shape=pltpu.HBM((rows, cells), BF16),
+        input_output_aliases={1: 0},
+        scratch_shapes=[dma((parts,))],
+        compiler_params=pltpu.CompilerParams(vmem_limit_bytes=4 * 1024 * 1024),
+        name="write_rest",
+    )(rest, out)
     return out.reshape(prior.shape)
 
 

time: 190 us -> 190 us (level)
  local copies, waits for them, and re-layouts: 3.4 us -> 0 us
  Pallas kernels: 186 us -> 188 us
    pallas_call x0 -> x3, Pallas kernels: none -> 23.8 us  [the longest x1 19.7 us: body(): pl.pallas_call(functools.partial(finish_kernel, parts), in_specs=[far, ne...]
    pallas_call x1, Pallas kernels: 186 us -> 165 us  [body(): pl.pallas_call(functools.partial(smoother_kernel, parts, tiles, times), i...]
    unnamed x1 -> x0, local copies, waits for them, and re-layouts: 3.4 us -> none
where the time goes in v5:
time: 190 us; the launch traced here: 188 us
  Pallas kernels  188 us (99%)
    pallas_call x1, Pallas kernels, body(): pl.pallas_call(functools.partial(smoother_kernel, parts, tiles, times), i...  165 us
    pallas_call x1, Pallas kernels, body(): pl.pallas_call(functools.partial(finish_kernel, parts), in_specs=[far, ne...  19.7 us

profile of v5, /device:TPU:0, one launch (start us, length us, event | category | flops | bytes accessed | tf_op | source)
XLA Modules:
  0.0 188.4 jit_solution(2882242511468082062)
XLA Ops:
  0.0 164.6 %smoother.1 = (bf16[128,24576]{1,0:T(8,128)(2,1)S(1)}, bf16[128,8192]{1,0:T(8,128)(2,1)S(1)}, bf16[1024,1024]{1,0:T(8,128)(2,1)S(1)}) custom-call(bf16[128,32768]{1,0:T(8,128)(2,1)} %bitcast.3, f32[1200]{0:T(1024)} %measured.1, f32[1200]{0:T(1024)} %noise.1, f32[2,64,1200]{2,1,0:T(8,128)} %bitcast.4, s32[2,1200]{1,0:T(2,128)} %couples.1, s32[1200]{0:T(1024)} %target.1), custom_call_target="tpu_custom_call" | custom-call | tf_op jit(solution)/shard_map/smoother/pallas_call | solution.py:547
  164.6 2.7 %write_most.1.out_early.before = bf16[128,32768]{1,0:T(8,128)(2,1)} custom-call(bf16[128,24576]{1,0:T(8,128)(2,1)S(1)} %get-tuple-element.8.piece), custom_call_target="tpu_custom_call" | custom-call | tf_op jit(solution)/shard_map/write_most/pallas_call | solution.py:562
  167.3 19.7 %finish.1.piece = bf16[128,8192]{1,0:T(8,128)(2,1)S(1)} custom-call(bf16[128,32768]{1,0:T(8,128)(2,1)} %write_most.1.out_early.before, bf16[128,8192]{1,0:T(8,128)(2,1)S(1)} %get-tuple-element.9.rest, bf16[1024,1024]{1,0:T(8,128)(2,1)S(1)} %get-tuple-element.10.last), custom_call_target="tpu_custom_call" | custom-call | tf_op jit(solution)/shard_map/finish/pallas_call | solution.py:571
  187.0 1.4 write_rest.1

commit v6 on v5

--- a/solution.py
+++ b/solution.py
@@ -11,7 +11,8 @@
 BLK = 64
 PASS_COUNT = 2
 LANES = 128
-CHUNKS = 4
+SHARES = (4, 4, 3, 5)
+CHUNKS = len(SHARES)
 F32 = jnp.float32
 BF16 = jnp.bfloat16
 HI = lax.Precision.HIGHEST
@@ -36,6 +37,10 @@
 
 def aligned(index, unit):
     return pl.ds(pl.multiple_of(index * unit, unit), unit)
+
+
+def spans(width):
+    return [width * part // sum(SHARES) for part in SHARES]
 
 
 def gauss_jordan(matrix, right, work):
@@ -115,7 +120,9 @@
     members = rows // times
     total_members = members * parts
     width = cells // parts
-    span = width // CHUNKS
+    size = spans(width)
+    first = [sum(size[:c]) for c in range(CHUNKS)]
+    tail = size[-1]
     obs = target.shape[0]
     padded = target_row.shape[1]
     share = padded // tiles
@@ -142,10 +149,10 @@
     own = pltpu.make_async_copy(prior.at[:, aligned(me, width)], state.at[pl.ds(0, rows), :], own_sem)
 
     def there(k, c):
-        column = pl.multiple_of((me ^ k) * width + c * span, span)
-        return pltpu.make_async_remote_copy(
-            src_ref=prior.at[:, pl.ds(column, span)],
-            dst_ref=state.at[pl.ds(k * rows, rows), pl.ds(c * span, span)],
+        column = pl.multiple_of((me ^ k) * width + first[c], LANES)
+        return pltpu.make_async_remote_copy(
+            src_ref=prior.at[:, pl.ds(column, size[c])],
+            dst_ref=state.at[pl.ds(k * rows, rows), pl.ds(first[c], size[c])],
             send_sem=there_send,
             recv_sem=there_recv.at[c],
             device_id={"mem": me ^ k},
@@ -153,10 +160,10 @@
         )
 
     def back(k, c):
-        column = pl.multiple_of(me * (width - span) + c * span, span)
-        return pltpu.make_async_remote_copy(
-            src_ref=state.at[pl.ds(k * rows, rows), pl.ds(c * span, span)],
-            dst_ref=out.at[:, pl.ds(column, span)],
+        column = pl.multiple_of(me * (width - tail) + first[c], LANES)
+        return pltpu.make_async_remote_copy(
+            src_ref=state.at[pl.ds(k * rows, rows), pl.ds(first[c], size[c])],
+            dst_ref=out.at[:, pl.ds(column, size[c])],
             send_sem=back_send,
             recv_sem=back_recv,
             device_id={"mem": me ^ k},
@@ -166,7 +173,7 @@
     def early(k):
         return pltpu.make_async_remote_copy(
             src_ref=last.at[pl.ds(k * rows, rows), :],
-            dst_ref=rest.at[:, aligned(me, span)],
+            dst_ref=rest.at[:, aligned(me, tail)],
             send_sem=early_send,
             recv_sem=early_recv,
             device_id={"mem": me ^ k},
@@ -352,27 +359,27 @@
     expand(solve(total, work), me, parts, times, mix)
 
     own.wait()
-    step = math.gcd(span, 256)
+    step = math.gcd(256, *size)
     depth = parts * rows
     for c in range(CHUNKS):
-        arrived = state.at[pl.ds(rows, depth - rows), pl.ds(c * span, span)]
+        arrived = state.at[pl.ds(rows, depth - rows), pl.ds(first[c], size[c])]
         whole(arrived, there_send, there_recv.at[c]).wait_recv()
 
         def update(i, carry):
-            columns = pl.ds(pl.multiple_of(c * span + i * step, step), step)
+            columns = pl.ds(pl.multiple_of(first[c] + i * step, step), step)
             x = state[:, columns]
             both = jnp.dot(mix[...], x, preferred_element_type=F32)
             y = (x.astype(F32) + both[:depth] + both[depth:]).astype(BF16)
             if c < CHUNKS - 1:
                 state[:, columns] = y
-                column = me * (width - span) + c * span + i * step
+                column = me * (width - tail) + first[c] + i * step
                 out[:, pl.ds(pl.multiple_of(column, step), step)] = y[:rows]
             else:
                 last[:, aligned(i, step)] = y
-                rest[:, pl.ds(pl.multiple_of(me * span + i * step, step), step)] = y[:rows]
+                rest[:, pl.ds(pl.multiple_of(me * tail + i * step, step), step)] = y[:rows]
             return carry
 
-        lax.fori_loop(0, span // step, update, 0)
+        lax.fori_loop(0, size[c] // step, update, 0)
         if c < CHUNKS - 1:
             for k in partners:
                 back(k, c).start()
@@ -385,7 +392,7 @@
             early(k).start()
 
     whole(state.at[pl.ds(rows, depth - rows), :], there_send, back_recv).wait_send()
-    moved = state.at[pl.ds(rows, depth - rows), pl.ds(0, width - span)]
+    moved = state.at[pl.ds(rows, depth - rows), pl.ds(0, width - tail)]
     whole(moved, back_send, back_recv).wait()
 
     @pl.when(odd)
@@ -428,12 +435,9 @@
             device_id_type=MESH,
         ).wait()
 
-    for k in evens:
-        signal(barrier, k)
-
     @pl.when(even)
     def _():
-        for k in odds:
+        for k in partners:
             signal(barrier, k)
         pl.semaphore_wait(barrier, len(evens))
         for k in evens:
@@ -442,7 +446,7 @@
 
     @pl.when(odd)
     def _():
-        pl.semaphore_wait(barrier, len(partners))
+        pl.semaphore_wait(barrier, len(odds))
         for k in odds:
             signal(go_sem, k)
 
@@ -542,7 +546,7 @@
         couples,
         target,
     )
-    span = width // CHUNKS
+    span = spans(width)[-1]
     near = pl.BlockSpec(memory_space=pltpu.VMEM)
     most, rest, last = pl.pallas_call(
         functools.partial(smoother_kernel, parts, tiles, times),

time: 190 us -> 188 us (0.989)
    pallas_call x1, Pallas kernels: 165 us -> 159 us  [body(): pl.pallas_call(functools.partial(smoother_kernel, parts, tiles, times), i...]
    pallas_call x1, Pallas kernels: 19.7 us -> 23.8 us  [body(): pl.pallas_call(functools.partial(finish_kernel, parts), in_specs=[far, ne...]
where the time goes in v6:
time: 188 us; the launch traced here: 187 us
  Pallas kernels  187 us (99%)
    pallas_call x1, Pallas kernels, body(): pl.pallas_call(functools.partial(smoother_kernel, parts, tiles, times), i...  159 us
    pallas_call x1, Pallas kernels, body(): pl.pallas_call(functools.partial(finish_kernel, parts), in_specs=[far, ne...  23.8 us

profile of v6, /device:TPU:0, one launch (start us, length us, event | category | flops | bytes accessed | tf_op | source)
XLA Modules:
  0.0 186.9 jit_solution(11744936130382063670)
XLA Ops:
  0.0 158.9 %smoother.1 = (bf16[128,22528]{1,0:T(8,128)(2,1)S(1)}, bf16[128,10240]{1,0:T(8,128)(2,1)S(1)}, bf16[1024,1280]{1,0:T(8,128)(2,1)S(1)}) custom-call(bf16[128,32768]{1,0:T(8,128)(2,1)} %bitcast.3, f32[1200]{0:T(1024)} %measured.1, f32[1200]{0:T(1024)} %noise.1, f32[2,64,1200]{2,1,0:T(8,128)} %bitcast.4, s32[2,1200]{1,0:T(2,128)} %couples.1, s32[1200]{0:T(1024)} %target.1), custom_call_target="tpu_custom_call" | custom-call | tf_op jit(solution)/shard_map/smoother/pallas_call | solution.py:551
  158.9 2.6 %write_most.1.out_early.before = bf16[128,32768]{1,0:T(8,128)(2,1)} custom-call(bf16[128,22528]{1,0:T(8,128)(2,1)S(1)} %get-tuple-element.8.piece), custom_call_target="tpu_custom_call" | custom-call | tf_op jit(solution)/shard_map/write_most/pallas_call | solution.py:566
  161.5 23.8 %finish.1.piece = bf16[128,10240]{1,0:T(8,128)(2,1)S(1)} custom-call(bf16[128,32768]{1,0:T(8,128)(2,1)} %write_most.1.out_early.before, bf16[128,10240]{1,0:T(8,128)(2,1)S(1)} %get-tuple-element.9.rest, bf16[1024,1280]{1,0:T(8,128)(2,1)S(1)} %get-tuple-element.10.last), custom_call_target="tpu_custom_call" | custom-call | tf_op jit(solution)/shard_map/finish/pallas_call | solution.py:575
  185.4 1.6 write_rest.1

commit v7 on v6

--- a/solution.py
+++ b/solution.py
@@ -400,9 +400,9 @@
         whole(last.at[pl.ds(0, len(evens) * rows), :], early_send, early_recv).wait()
 
 
-def finish_kernel(parts, out_early, rest, last, out, send_sem, recv_sem, go_sem):
+def finish_kernel(parts, before, last, out, send_sem, recv_sem, go_sem):
     me = lax.axis_index("mem")
-    rows = rest.shape[0]
+    rows = out.shape[0]
     span = last.shape[1]
     partners = list(reversed(range(1, parts)))
     evens = partners[1::2]
@@ -452,12 +452,9 @@
 
     for k in odds:
         copy(k).start()
-    out[:, aligned(me, span)] = rest[:, aligned(me, span)]
 
     @pl.when(odd)
     def _():
-        for k in evens:
-            out[:, aligned(me ^ k, span)] = rest[:, aligned(me ^ k, span)]
         settle(len(odds))
 
     @pl.when(even)
@@ -465,20 +462,52 @@
         settle(len(partners))
 
 
-def write_kernel(parts, width, offset, piece, out, sem):
-    size = piece.shape[1] // parts
-    copies = [
-        pltpu.make_async_copy(
-            piece.at[:, pl.ds(i * size, size)],
-            out.at[:, pl.ds(i * width + offset, size)],
-            sem.at[i],
-        )
-        for i in range(parts)
-    ]
+def run(copies):
     for copy in copies:
         copy.start()
     for copy in copies:
         copy.wait()
+
+
+def tail_piece(k, width, rest, out, sem):
+    owner = lax.axis_index("mem") ^ k
+    span = rest.shape[1] * width // out.shape[1]
+    column = pl.multiple_of(owner * width + width - span, LANES)
+    return pltpu.make_async_copy(
+        rest.at[:, aligned(owner, span)], out.at[:, pl.ds(column, span)], sem.at[k]
+    )
+
+
+def write_most_kernel(parts, width, most, rest, out, sem, tail_sem):
+    size = most.shape[1] // parts
+    copies = [
+        pltpu.make_async_copy(
+            most.at[:, pl.ds(i * size, size)], out.at[:, pl.ds(i * width, size)], sem.at[i]
+        )
+        for i in range(parts)
+    ]
+    copies.append(tail_piece(0, width, rest, out, tail_sem))
+    for copy in copies:
+        copy.start()
+
+    @pl.when(lax.rem(lax.axis_index("mem"), 2) == 1)
+    def _():
+        run([tail_piece(k, width, rest, out, tail_sem) for k in range(2, parts, 2)])
+
+    for copy in copies:
+        copy.wait()
+
+
+def write_rest_kernel(parts, width, rest, before, out, sem):
+    odd = lax.rem(lax.axis_index("mem"), 2) == 1
+
+    @pl.when(odd)
+    def _():
+        run([tail_piece(k, width, rest, out, sem) for k in range(1, parts, 2)])
+
+    @pl.when(jnp.logical_not(odd))
+    def _():
+        run([tail_piece(k, width, rest, out, sem) for k in range(1, parts)])
 
 
 def body(prior, measured, noise, jitter, couples, target):
@@ -564,17 +593,17 @@
         name="smoother",
     )(*(pltpu.with_memory_space_constraint(a, pltpu.HBM) for a in operands))
     out = pl.pallas_call(
-        functools.partial(write_kernel, parts, width, 0),
-        in_specs=[near],
+        functools.partial(write_most_kernel, parts, width),
+        in_specs=[near, near],
         out_specs=far,
         out_shape=pltpu.HBM((rows, cells), BF16),
-        scratch_shapes=[dma((parts,))],
+        scratch_shapes=[dma((parts,)), dma((parts,))],
         compiler_params=pltpu.CompilerParams(vmem_limit_bytes=4 * 1024 * 1024),
         name="write_most",
-    )(most)
+    )(most, rest)
     rest = pl.pallas_call(
         functools.partial(finish_kernel, parts),
-        in_specs=[far, near, near],
+        in_specs=[far, near],
         out_specs=near,
         out_shape=pltpu.VMEM((rows, parts * span), BF16),
         scratch_shapes=[dma, dma, pltpu.SemaphoreType.REGULAR],
@@ -582,13 +611,9 @@
             collective_id=1, has_side_effects=True, vmem_limit_bytes=8 * 1024 * 1024
         ),
         name="finish",
-    )(pltpu.with_memory_space_constraint(out, pltpu.HBM), rest, last)
-
-    def write_rest(piece, before, after, sem):
-        write_kernel(parts, width, width - span, piece, after, sem)
-
+    )(pltpu.with_memory_space_constraint(out, pltpu.HBM), last)
     out = pl.pallas_call(
-        write_rest,
+        functools.partial(write_rest_kernel, parts, width),
         in_specs=[near, far],
         out_specs=far,
         out_shape=pltpu.HBM((rows, cells), BF16),

time: 188 us -> 188 us (level)
  no operation moved by 1% of the time
where the time goes in v7:
time: 188 us; the launch traced here: 187 us
  Pallas kernels  187 us (99%)
    pallas_call x1, Pallas kernels, body(): pl.pallas_call(functools.partial(smoother_kernel, parts, tiles, times), i...  159 us
    pallas_call x1, Pallas kernels, body(): pl.pallas_call(functools.partial(finish_kernel, parts), in_specs=[far, ne...  23.8 us

profile of v7, /device:TPU:0, one launch (start us, length us, event | category | flops | bytes accessed | tf_op | source)
XLA Modules:
  0.0 187.0 jit_solution(13622472251141673827)
XLA Ops:
  0.0 158.9 %smoother.1 = (bf16[128,22528]{1,0:T(8,128)(2,1)S(1)}, bf16[128,10240]{1,0:T(8,128)(2,1)S(1)}, bf16[1024,1280]{1,0:T(8,128)(2,1)S(1)}) custom-call(bf16[128,32768]{1,0:T(8,128)(2,1)} %bitcast.3, f32[1200]{0:T(1024)} %measured.1, f32[1200]{0:T(1024)} %noise.1, f32[2,64,1200]{2,1,0:T(8,128)} %bitcast.4, s32[2,1200]{1,0:T(2,128)} %couples.1, s32[1200]{0:T(1024)} %target.1), custom_call_target="tpu_custom_call" | custom-call | tf_op jit(solution)/shard_map/smoother/pallas_call | solution.py:580
  158.9 2.7 %write_most.1.before = bf16[128,32768]{1,0:T(8,128)(2,1)} custom-call(bf16[128,22528]{1,0:T(8,128)(2,1)S(1)} %get-tuple-element.8.most, bf16[128,10240]{1,0:T(8,128)(2,1)S(1)} %get-tuple-element.9.rest), custom_call_target="tpu_custom_call" | custom-call | tf_op jit(solution)/shard_map/write_most/pallas_call | solution.py:595
  161.7 23.8 %finish.1.rest = bf16[128,10240]{1,0:T(8,128)(2,1)S(1)} custom-call(bf16[128,32768]{1,0:T(8,128)(2,1)} %write_most.1.before, bf16[1024,1280]{1,0:T(8,128)(2,1)S(1)} %get-tuple-element.10.last), custom_call_target="tpu_custom_call" | custom-call | tf_op jit(solution)/shard_map/finish/pallas_call | solution.py:604
  185.5 1.5 write_rest.1

commit v8 on v7

--- a/solution.py
+++ b/solution.py
@@ -233,7 +233,7 @@
             device_id_type=MESH,
         )
 
-    partners = list(reversed(range(1, parts)))
+    partners = list(range(1, parts))
     evens = partners[1::2]
     others = list(range(1, tiles))
 

time: 188 us -> 187 us (level)
  no operation moved by 1% of the time
where the time goes in v8:
time: 187 us
  Pallas kernels  187 us (100%)
    pallas_call x1, Pallas kernels, body(): pl.pallas_call(functools.partial(smoother_kernel, parts, tiles, times), i...  158 us
    pallas_call x1, Pallas kernels, body(): pl.pallas_call(functools.partial(finish_kernel, parts), in_specs=[far, ne...  24.7 us

profile of v8, /device:TPU:0, one launch (start us, length us, event | category | flops | bytes accessed | tf_op | source)
XLA Modules:
  0.0 186.9 jit_solution(17606145718111969241)
XLA Ops:
  0.0 158.0 %smoother.1 = (bf16[128,22528]{1,0:T(8,128)(2,1)S(1)}, bf16[128,10240]{1,0:T(8,128)(2,1)S(1)}, bf16[1024,1280]{1,0:T(8,128)(2,1)S(1)}) custom-call(bf16[128,32768]{1,0:T(8,128)(2,1)} %bitcast.3, f32[1200]{0:T(1024)} %measured.1, f32[1200]{0:T(1024)} %noise.1, f32[2,64,1200]{2,1,0:T(8,128)} %bitcast.4, s32[2,1200]{1,0:T(2,128)} %couples.1, s32[1200]{0:T(1024)} %target.1), custom_call_target="tpu_custom_call" | custom-call | tf_op jit(solution)/shard_map/smoother/pallas_call | solution.py:580
  158.0 2.7 %write_most.1.before = bf16[128,32768]{1,0:T(8,128)(2,1)} custom-call(bf16[128,22528]{1,0:T(8,128)(2,1)S(1)} %get-tuple-element.8.most, bf16[128,10240]{1,0:T(8,128)(2,1)S(1)} %get-tuple-element.9.rest), custom_call_target="tpu_custom_call" | custom-call | tf_op jit(solution)/shard_map/write_most/pallas_call | solution.py:595
  160.7 24.7 %finish.1.rest = bf16[128,10240]{1,0:T(8,128)(2,1)S(1)} custom-call(bf16[128,32768]{1,0:T(8,128)(2,1)} %write_most.1.before, bf16[1024,1280]{1,0:T(8,128)(2,1)S(1)} %get-tuple-element.10.last), custom_call_target="tpu_custom_call" | custom-call | tf_op jit(solution)/shard_map/finish/pallas_call | solution.py:604
  185.4 1.5 write_rest.1

commit v9 on v8

--- a/solution.py
+++ b/solution.py
@@ -240,9 +240,6 @@
     barrier = pltpu.get_barrier_semaphore()
     for k in partners:
         pl.semaphore_signal(barrier, inc=1, device_id={"mem": me ^ k}, device_id_type=MESH)
-    look_copy(0).start()
-    for load in loads:
-        load.start()
 
     speaker = me == parts - 1
     root = jnp.logical_and(speaker, tile == tiles - 1)
@@ -267,6 +264,9 @@
 
     for k in partners:
         there(k, 0).start()
+    look_copy(0).start()
+    for load in loads:
+        load.start()
     own.start()
 
     summer[...] = (iota((look, LANES), 0) // BLK == iota((look, LANES), 1)).astype(BF16)

time: 187 us -> 187 us (level)
  no operation moved by 1% of the time
where the time goes in v9:
time: 187 us
  Pallas kernels  187 us (100%)
    pallas_call x1, Pallas kernels, body(): pl.pallas_call(functools.partial(smoother_kernel, parts, tiles, times), i...  158 us
    pallas_call x1, Pallas kernels, body(): pl.pallas_call(functools.partial(finish_kernel, parts), in_specs=[far, ne...  24.7 us

profile of v9, /device:TPU:0, one launch (start us, length us, event | category | flops | bytes accessed | tf_op | source)
XLA Modules:
  0.0 186.9 jit_solution(8510681378598033612)
XLA Ops:
  0.0 158.0 %smoother.1 = (bf16[128,22528]{1,0:T(8,128)(2,1)S(1)}, bf16[128,10240]{1,0:T(8,128)(2,1)S(1)}, bf16[1024,1280]{1,0:T(8,128)(2,1)S(1)}) custom-call(bf16[128,32768]{1,0:T(8,128)(2,1)} %bitcast.3, f32[1200]{0:T(1024)} %measured.1, f32[1200]{0:T(1024)} %noise.1, f32[2,64,1200]{2,1,0:T(8,128)} %bitcast.4, s32[2,1200]{1,0:T(2,128)} %couples.1, s32[1200]{0:T(1024)} %target.1), custom_call_target="tpu_custom_call" | custom-call | tf_op jit(solution)/shard_map/smoother/pallas_call | solution.py:580
  158.0 2.7 %write_most.1.before = bf16[128,32768]{1,0:T(8,128)(2,1)} custom-call(bf16[128,22528]{1,0:T(8,128)(2,1)S(1)} %get-tuple-element.8.most, bf16[128,10240]{1,0:T(8,128)(2,1)S(1)} %get-tuple-element.9.rest), custom_call_target="tpu_custom_call" | custom-call | tf_op jit(solution)/shard_map/write_most/pallas_call | solution.py:595
  160.7 24.7 %finish.1.rest = bf16[128,10240]{1,0:T(8,128)(2,1)S(1)} custom-call(bf16[128,32768]{1,0:T(8,128)(2,1)} %write_most.1.before, bf16[1024,1280]{1,0:T(8,128)(2,1)S(1)} %get-tuple-element.10.last), custom_call_target="tpu_custom_call" | custom-call | tf_op jit(solution)/shard_map/finish/pallas_call | solution.py:604
  185.4 1.5 write_rest.1
